TPU v7x, 32 devices: a whole 2x2x4 slice. The times are simulated.
32 devices in a mesh: groups: 2 (over y), expert: 16 (over z, x, core).
Axes of the slice: x: 2, y: 2, z: 4, core: 2. Of those that a mesh axis runs over, the one named last changes fastest.
Arguments:
- attn_heads: bfloat16 [4096, 4096], P(('groups', 'expert')), parts along dimension 0, may hold values from -6 to 6
- residual: bfloat16 [4096, 2048], P(('groups', 'expert')), parts along dimension 0, may hold values from -6 to 6
- w_out: bfloat16 [4096, 2048], P('expert'), may hold values from -0.09375 to 0.09375
- norm_gain: float32 [2048], replicated, may hold values from 0.1 to 1.9
- expert_ids: int32 [4096, 8], P(('groups', 'expert')), parts along dimension 0, may hold values from 0 to 15, all different within a row; in each aligned block of 128 rows (0 to 127, 128 to 255, ...) at most 80 rows name the same one
- route_num: int32 [4096, 8], P(('groups', 'expert')), parts along dimension 0, may hold values from 1 to 16
- w_gate: bfloat16 [16, 2048, 768], P('expert'), may hold values from -0.125 to 0.125
- w_up: bfloat16 [16, 2048, 768], P('expert'), may hold values from -0.125 to 0.125
- w_down: bfloat16 [16, 768, 2048], P('expert'), may hold values from -0.21875 to 0.21875
Outputs:
- mid_state: bfloat16 [4096, 2048], P(('groups', 'expert')), parts along dimension 0
- expert_out: bfloat16 [4096, 2048], P(('groups', 'expert')), parts along dimension 0
There are 2 independent parts, one for each index of `groups`. A program takes and returns all parts, laid end to end along the dimension named above; an argument that names none is the same for every part. Nothing has to cross between parts.
Inputs may be any that keep to these rules, and one draw needn't show every extreme that they name: `expert_ids`: each token names 8 different experts; among the 128 tokens of one device no expert is named more than 80 times, a bound that some block reaches.
All inputs are finite; a program needn't handle non-finite values.
Results may differ from a plain program's by a relative error of at most 0.0095.
Values may be sent and summed in bfloat16 or wider, within the bound.
No kernel may reach another device: no remote copies, remote signals or barrier semaphores. Data moves between devices by JAX's collectives and lax.ppermute only.
A program may use at most 128 MiB of HBM per device.

v0:
```python
import jax
import jax.numpy as jnp
from jax import lax
from jax.sharding import PartitionSpec as P

epsilon = 1e-06


def rms_scale(tensor, norm_gain):
    values = tensor.astype(jnp.float32)
    mean_sq = jnp.mean(values * values, axis=-1, keepdims=True)
    return (values * lax.rsqrt(mean_sq + epsilon) * norm_gain).astype(jnp.bfloat16)


def per_device(attn_heads, residual, w_out, norm_gain, expert_ids, route_num, w_gate, w_up, w_down):
    tok_rows = attn_heads.shape[0]
    feature_count = residual.shape[1]
    gathered = lax.all_gather(w_out, "expert", axis=0, tiled=True)
    projected = jnp.dot(attn_heads, gathered, preferred_element_type=jnp.float32)
    mid_state = (residual.astype(jnp.float32) + projected).astype(jnp.bfloat16)
    n_experts = lax.axis_size("expert")
    top_count = expert_ids.shape[1]
    capacity = tok_rows * top_count * 5 // (4 * n_experts)
    flat_ids = expert_ids.reshape(-1)
    onehot = (flat_ids[:, None] == jnp.arange(n_experts, dtype=jnp.int32)[None, :]).astype(
        jnp.int32
    )
    before = jnp.cumsum(onehot, axis=0) - onehot
    slot_index = jnp.sum(before * onehot, axis=1)
    position = flat_ids * capacity + slot_index
    token_index = jnp.arange(tok_rows * top_count, dtype=jnp.int32) // top_count
    payload = rms_scale(mid_state, norm_gain)
    sendbuf = jnp.zeros((n_experts * capacity, feature_count), jnp.bfloat16)
    sendbuf = sendbuf.at[position].set(payload[token_index])
    sendbuf = sendbuf.reshape(n_experts, capacity, feature_count)
    received = lax.all_to_all(sendbuf, "expert", split_axis=0, concat_axis=0, tiled=True)
    sources, slot_count, _ = received.shape
    row_block = received.reshape(sources * slot_count, feature_count)
    gate_act = jnp.dot(row_block, w_gate[0], preferred_element_type=jnp.float32)
    up_act = jnp.dot(row_block, w_up[0], preferred_element_type=jnp.float32)
    hidden = (jax.nn.silu(gate_act) * up_act).astype(jnp.bfloat16)
    result = jnp.dot(hidden, w_down[0], preferred_element_type=jnp.float32).astype(jnp.bfloat16)
    result = result.reshape(sources, slot_count, feature_count)
    returned = lax.all_to_all(result, "expert", split_axis=0, concat_axis=0, tiled=True)
    returned = returned.reshape(n_experts * capacity, feature_count)
    picked = returned[position].astype(jnp.float32).reshape(tok_rows, top_count, feature_count)
    numer = route_num.astype(jnp.float32)
    weights = numer / jnp.sum(numer, axis=1, keepdims=True)
    expert_out = jnp.sum(picked * weights[:, :, None], axis=1).astype(jnp.bfloat16)
    return (mid_state, expert_out)


def solution(mesh):
    in_specs = (
        P(("groups", "expert"), None),
        P(("groups", "expert"), None),
        P("expert", None),
        P(),
        P(("groups", "expert"), None),
        P(("groups", "expert"), None),
        P("expert", None, None),
        P("expert", None, None),
        P("expert", None, None),
    )
    out_specs = (P(("groups", "expert"), None), P(("groups", "expert"), None))
    return jax.shard_map(
        per_device, mesh=mesh, in_specs=in_specs, out_specs=out_specs, check_vma=False
    )
```

profile of v0, /device:TPU:11, one launch (start us, length us, event | category | flops | bytes accessed | tf_op | source)
XLA Modules:
  0.0 452.5 jit_solution(2157559371774095986)
XLA Ops:
  7.2 0.7 all-gather.2.cloned.1.call-update
  7.9 1.0 copy.15
  8.9 0.1 eq.29
  9.0 0.1 eq.25
  9.1 0.7 broadcast_multiply_fusion
  9.8 0.1 copy.14
  9.9 0.1 mul.55
  10.0 4.5 reduce-window.6
  14.6 0.1 copy.17
  14.8 0.1 broadcast_add_fusion
  15.0 120.6 %all-gather.2.cloned.1.call-done = bf16[4096,2048]{1,0:T(8,128)(2,1)} async-done(((bf16[256,2048]{1,0:T(8,128)(2,1)}), bf16[4096,2048]{1,0:T(8,128)(2,1)}) %all-gather.2.cloned.1.call-update) | async-done | bytes 16777232 | tf_op jit(solution)/shard_map/all_gather | solution.py:18
  135.6 8.6 %fusion.10 = (f32[128]{0:T(128)S(1)}, bf16[128,2048]{1,0:T(8,128)(2,1)S(1)}) fusion(bf16[128,4096]{1,0:T(8,128)(2,1)} %param.9, bf16[4096,2048]{1,0:T(8,128)(2,1)} %all-gather.2.cloned.1.call-done, bf16[128,2048]{1,0:T(8,128)(2,1)} %param.10), kind=kOutput, calls=%fused_computation.19 | convolution fusion | flops 2149056512 | bytes 18874880 | tf_op jit(solution)/shard_map/dot_general | solution.py:19
  144.2 0.8 copy-done.1
  145.0 1.0 fusion.12
  146.0 23.5 %scatter_custom_fusion = bf16[1280,2048]{1,0:T(8,128)(2,1)} fusion(s32[1024]{0:T(1024)S(1)} %bitcast.50, bf16[128,2048]{1,0:T(8,128)(2,1)} %fusion.12, s32[1024]{0:T(1024)S(1)} %broadcast_clamp_fusion.1, bf16[]{:T(256)} %constant.29.clone.1), kind=kCustom, calls=%fused_computation.6 | custom fusion | bytes 5243392 | tf_op jit(solution)/shard_map/scatter | solution.py:34
  169.5 121.6 %all_to_all.10 = bf16[16,80,2048]{2,1,0:T(8,128)(2,1)S(1)} all-to-all(bf16[16,80,2048]{2,1,0:T(8,128)(2,1)} %bitcast.43), channel_id=1, replica_groups=mesh['groups'=2,'expert'=16] {'expert'}, dimensions={0} | all-to-all | bytes 10485760 | tf_op jit(solution)/shard_map/all_to_all | solution.py:36
  291.1 4.3 fusion.6
  295.4 4.8 %fusion.3 = bf16[1280,768]{1,0:T(8,128)(2,1)S(1)} fusion(bf16[1280,2048]{1,0:T(8,128)(2,1)S(1)} %bitcast.46, f32[1280,768]{1,0:T(8,128)S(1)} %fusion.6, bf16[1,2048,768]{2,1,0:T(8,128)(2,1)S(1)} %copy-done.5), kind=kOutput, calls=%fused_computation.9 | convolution fusion | flops 4032430080 | bytes 14286848 | tf_op jit(solution)/shard_map/dot_general | solution.py:40
  300.2 6.1 %convolution_convert_fusion = bf16[1280,2048]{1,0:T(8,128)(2,1)} fusion(bf16[1280,768]{1,0:T(8,128)(2,1)S(1)} %fusion.3, bf16[1,768,2048]{2,1,0:T(8,128)(2,1)S(1)} %copy-done), kind=kOutput, calls=%fused_computation.5 | convolution fusion | flops 4029153280 | bytes 10354688 | tf_op jit(solution)/shard_map/dot_general | solution.py:42
  306.3 5.1 %all-to-all-start.1 = ((bf16[16,80,2048]{2,1,0:T(8,128)(2,1)}), bf16[16,80,2048]{2,1,0:T(8,128)(2,1)}, u32[]{:S(2)}, u32[]{:S(2)}) async-start(bf16[16,80,2048]{2,1,0:T(8,128)(2,1)} %bitcast.44), calls=%async_computation.1 | async-start | bytes 10485760 | tf_op jit(solution)/shard_map/all_to_all | solution.py:44
  311.4 0.1 copy.19
  311.5 114.8 %all-to-all-done.1 = bf16[16,80,2048]{2,1,0:T(8,128)(2,1)} async-done(((bf16[16,80,2048]{2,1,0:T(8,128)(2,1)}), bf16[16,80,2048]{2,1,0:T(8,128)(2,1)}, u32[]{:S(2)}, u32[]{:S(2)}) %all-to-all-start.1) | async-done | bytes 5242912 | tf_op jit(solution)/shard_map/all_to_all | solution.py:44
  426.3 12.0 %gather_fusion = bf16[1024,2048]{1,0:T(8,128)(2,1)} fusion(bf16[1280,2048]{1,0:T(8,128)(2,1)} %bitcast.11, s32[1024]{0:T(1024)S(1)} %broadcast_clamp_fusion), kind=kCustom, calls=%fused_computation.1 | custom fusion | bytes 8392704 | tf_op jit(solution)/shard_map/gather | solution.py:46
  438.4 7.3 %fusion = bf16[128,2048]{1,0:T(8,128)(2,1)} fusion(bf16[1024,2048]{1,0:T(8,128)(2,1)} %gather_fusion, f32[128,8]{1,0:T(8,128)S(1)} %copy.19), kind=kLoop, calls=%fused_computation.4 | loop fusion | flops 6029312 | bytes 4722688 | tf_op jit(solution)/shard_map/reduce_sum | solution.py:49
  (25 shorter events, 0.3 us)
Async XLA Ops:
  7.2 293.1 %copy-start = (bf16[1,768,2048]{2,1,0:T(8,128)(2,1)S(1)}, bf16[1,768,2048]{2,1,0:T(8,128)(2,1)}, u32[]{:S(2)}) copy-start(bf16[1,768,2048]{2,1,0:T(8,128)(2,1)} %param.17) | copy-start | bytes 9437188
  7.2 128.4 %all-gather.2.cloned.1.call-start = ((), (), s32[]{:S(2)}) async-start(), calls=%async_computation.2 | async-start | bytes 17825792 | tf_op jit(solution)/shard_map/all_gather | solution.py:18
  15.0 130.0 %copy-start.3 = (f32[2048]{0:T(1024)S(1)}, f32[2048]{0:T(1024)}, u32[]{:S(2)}) copy-start(f32[2048]{0:T(1024)} %param.12) | copy-start | bytes 24580
  144.2 0.8 copy-start.1
  169.5 121.6 %copy-start.4 = (bf16[1,2048,768]{2,1,0:T(8,128)(2,1)S(1)}, bf16[1,2048,768]{2,1,0:T(8,128)(2,1)}, u32[]{:S(2)}) copy-start(bf16[1,2048,768]{2,1,0:T(8,128)(2,1)} %param.15) | copy-start | bytes 9437188
  291.1 4.3 copy-start.5
  306.3 5.1 %copy-start.2 = (s32[128,8]{0,1:T(8,128)S(1)}, s32[128,8]{0,1:T(8,128)}, u32[]{:S(2)}) copy-start(s32[128,8]{0,1:T(8,128)} %param.14) | copy-start | bytes 12292
  306.3 120.0 %all-to-all-start.1 = ((bf16[16,80,2048]{2,1,0:T(8,128)(2,1)}), bf16[16,80,2048]{2,1,0:T(8,128)(2,1)}, u32[]{:S(2)}, u32[]{:S(2)}) async-start(bf16[16,80,2048]{2,1,0:T(8,128)(2,1)} %bitcast.44), calls=%async_computation.1 | async-start | bytes 10485760 | tf_op jit(solution)/shard_map/all_to_all | solution.py:44
Sparse Core Ops, SparseCore 0:
  10.2 125.3 all-gather.1
where the time goes:
time: 453 us
  waiting for transfers between devices  236 us (52%)
  blocking collectives  122 us (27%)
  local copies, waits for them, and re-layouts  38.1 us (8%)
  matrix products  23.8 us (5%)
  between operations  14.2 us (3%)
  other arithmetic  13.7 us (3%)
  starting transfers between devices  5.1 us (1%)
    all_to_all x1, blocking collectives, per_device(): lax.all_to_all(sendbuf, 'expert', split_axis=0, concat_axis=0, tiled=True)  122 us
    all_gather x1, waiting for transfers between devices, per_device(): gathered = lax.all_gather(w_out, 'expert', axis=0, tiled=True)  121 us
    all_to_all x1, waiting for transfers between devices, per_device(): lax.all_to_all(result, 'expert', split_axis=0, concat_axis=0, tiled=True)  115 us
    scatter x1, local copies, waits for them, and re-layouts, per_device(): sendbuf = sendbuf.at[position].set(payload[token_index])  23.5 us
    gather x1, local copies, waits for them, and re-layouts, per_device(): returned[position].astype(jnp.float32)  12 us
  transfers between devices with their start and end apart: 2, of which 2 were waited for; matrix products, arithmetic and copies ran while one was open for 2% of the time, Pallas kernels for 0%

commit v1 on v0

--- a/solution.py
+++ b/solution.py
@@ -15,7 +15,9 @@
 def per_device(attn_heads, residual, w_out, norm_gain, expert_ids, route_num, w_gate, w_up, w_down):
     tok_rows = attn_heads.shape[0]
     feature_count = residual.shape[1]
-    gathered = lax.all_gather(w_out, "expert", axis=0, tiled=True)
+    gathered = jnp.concatenate(
+        lax.all_to_all(jnp.stack([w_out] * lax.axis_size("expert")), "expert", 0, 0), axis=0
+    )
     projected = jnp.dot(attn_heads, gathered, preferred_element_type=jnp.float32)
     mid_state = (residual.astype(jnp.float32) + projected).astype(jnp.bfloat16)
     n_experts = lax.axis_size("expert")

time: 453 us -> 686 us (1.51)
  waiting for transfers between devices: 236 us -> 471 us
  between operations: 14.2 us -> 0.77 us
  starting transfers between devices: 5.1 us -> 12.1 us
    all_to_all x0 -> x1, waiting for transfers between devices: none -> 357 us  [per_device(): lax.all_to_all(jnp.stack([w_out] * lax.axis_size('expert')), 'expert', 0, 0)]
    all_gather x1 -> x0, waiting for transfers between devices: 121 us -> none  [per_device(): gathered = lax.all_gather(w_out, 'expert', axis=0, tiled=True)]
    another operation x2 -> x3, local copies, waits for them, and re-layouts: 0.08 us -> 7.09 us  [the longest x1 7.01 us: per_device(): jnp.stack([w_out] * lax.axis_size('expert'))]
  transfers between devices with their start and end apart: 2 -> 2, of which waited for: 2 -> 2; matrix products, arithmetic and copies ran while one was open for 2% -> 1% of each run, Pallas kernels for 0% -> 0%
where the time goes in v1:
time: 686 us; the launch traced here: 685 us
  waiting for transfers between devices  471 us (69%)
  blocking collectives  120 us (17%)
  local copies, waits for them, and re-layouts  44.3 us (6%)
  matrix products  23.8 us (3%)
  other arithmetic  13 us (2%)
  starting transfers between devices  12.1 us (2%)
    all_to_all x1, waiting for transfers between devices, per_device(): lax.all_to_all(jnp.stack([w_out] * lax.axis_size('expert')), 'expert', 0, 0)  357 us
    all_to_all x1, blocking collectives, per_device(): lax.all_to_all(sendbuf, 'expert', split_axis=0, concat_axis=0, tiled=True)  120 us
    all_to_all x1, waiting for transfers between devices, per_device(): lax.all_to_all(result, 'expert', split_axis=0, concat_axis=0, tiled=True)  115 us
    scatter x1, local copies, waits for them, and re-layouts, per_device(): sendbuf = sendbuf.at[position].set(payload[token_index])  23.6 us
  transfers between devices with their start and end apart: 2, of which 2 were waited for; matrix products, arithmetic and copies ran while one was open for 1% of the time, Pallas kernels for 0%

profile of v1, /device:TPU:11, one launch (start us, length us, event | category | flops | bytes accessed | tf_op | source)
XLA Modules:
  0.0 685.1 jit_solution(15903869532167235633)
XLA Ops:
  0.6 7.0 %stack.2 = bf16[16,256,2048]{2,1,0:T(8,128)(2,1)} broadcast(bf16[256,2048]{1,0:T(8,128)(2,1)} %param.11), dimensions={1,2} | broadcast | bytes 17825792 | tf_op jit(solution)/shard_map/stack | solution.py:19
  7.7 6.7 all-to-all-start
  14.3 0.1 copy.15
  14.4 0.1 eq.29
  14.5 0.1 eq.25
  14.6 0.1 copy.14
  14.7 0.1 mul.55
  14.8 4.5 reduce-window.6
  19.4 0.1 copy.17
  19.7 0.1 broadcast_add_fusion
  19.8 356.6 %all-to-all-done = bf16[16,256,2048]{2,1,0:T(8,128)(2,1)} async-done(((bf16[16,256,2048]{2,1,0:T(8,128)(2,1)}), bf16[16,256,2048]{2,1,0:T(8,128)(2,1)}, u32[]{:S(2)}, u32[]{:S(2)}) %all-to-all-start) | async-done | bytes 16777248 | tf_op jit(solution)/shard_map/all_to_all | solution.py:19
  376.4 8.6 %fusion.10 = (f32[128]{0:T(128)S(1)}, bf16[128,2048]{1,0:T(8,128)(2,1)S(1)}) fusion(bf16[128,4096]{1,0:T(8,128)(2,1)} %param.9, bf16[4096,2048]{1,0:T(8,128)(2,1)} %bitcast, bf16[128,2048]{1,0:T(8,128)(2,1)} %param.10), kind=kOutput, calls=%fused_computation.19 | convolution fusion | flops 2149056512 | bytes 18874880 | tf_op jit(solution)/shard_map/dot_general | solution.py:21
  385.1 0.8 copy-done.1
  385.9 1.0 fusion.12
  386.8 23.6 %scatter_custom_fusion = bf16[1280,2048]{1,0:T(8,128)(2,1)} fusion(s32[1024]{0:T(1024)S(1)} %bitcast.50, bf16[128,2048]{1,0:T(8,128)(2,1)} %fusion.12, s32[1024]{0:T(1024)S(1)} %broadcast_clamp_fusion.1, bf16[]{:T(256)} %constant.29.clone.1), kind=kCustom, calls=%fused_computation.6 | custom fusion | bytes 5243392 | tf_op jit(solution)/shard_map/scatter | solution.py:36
  410.4 119.7 %all_to_all.15 = bf16[16,80,2048]{2,1,0:T(8,128)(2,1)S(1)} all-to-all(bf16[16,80,2048]{2,1,0:T(8,128)(2,1)} %bitcast.43), channel_id=1, replica_groups=mesh['groups'=2,'expert'=16] {'expert'}, dimensions={0} | all-to-all | bytes 10485760 | tf_op jit(solution)/shard_map/all_to_all | solution.py:38
  530.2 4.3 fusion.6
  534.5 4.8 fusion.3
  539.3 6.1 convolution_convert_fusion
  545.4 5.4 all-to-all-start.2
  550.8 0.1 copy.19
  551.0 114.8 %all-to-all-done.2 = bf16[16,80,2048]{2,1,0:T(8,128)(2,1)} async-done(((bf16[16,80,2048]{2,1,0:T(8,128)(2,1)}), bf16[16,80,2048]{2,1,0:T(8,128)(2,1)}, u32[]{:S(2)}, u32[]{:S(2)}) %all-to-all-start.2) | async-done | bytes 5242912 | tf_op jit(solution)/shard_map/all_to_all | solution.py:46
  665.7 12.0 %gather_fusion = bf16[1024,2048]{1,0:T(8,128)(2,1)} fusion(bf16[1280,2048]{1,0:T(8,128)(2,1)} %bitcast.12, s32[1024]{0:T(1024)S(1)} %broadcast_clamp_fusion), kind=kCustom, calls=%fused_computation.1 | custom fusion | bytes 8392704 | tf_op jit(solution)/shard_map/gather | solution.py:48
  677.8 7.3 %fusion = bf16[128,2048]{1,0:T(8,128)(2,1)} fusion(bf16[1024,2048]{1,0:T(8,128)(2,1)} %gather_fusion, f32[128,8]{1,0:T(8,128)S(1)} %copy.19), kind=kLoop, calls=%fused_computation.4 | loop fusion | flops 6029312 | bytes 4722688 | tf_op jit(solution)/shard_map/reduce_sum | solution.py:51
  (27 shorter events, 0.3 us)
Async XLA Ops:
  0.6 538.7 %copy-start = (bf16[1,768,2048]{2,1,0:T(8,128)(2,1)S(1)}, bf16[1,768,2048]{2,1,0:T(8,128)(2,1)}, u32[]{:S(2)}) copy-start(bf16[1,768,2048]{2,1,0:T(8,128)(2,1)} %param.17) | copy-start | bytes 9437188
  7.7 6.7 copy-start.2
  7.7 368.8 %all-to-all-start = ((bf16[16,256,2048]{2,1,0:T(8,128)(2,1)}), bf16[16,256,2048]{2,1,0:T(8,128)(2,1)}, u32[]{:S(2)}, u32[]{:S(2)}) async-start(bf16[16,256,2048]{2,1,0:T(8,128)(2,1)} %stack.2), calls=%async_computation | async-start | bytes 33554432 | tf_op jit(solution)/shard_map/all_to_all | solution.py:19
  376.4 9.4 %copy-start.4 = (f32[2048]{0:T(1024)S(1)}, f32[2048]{0:T(1024)}, u32[]{:S(2)}) copy-start(f32[2048]{0:T(1024)} %param.12) | copy-start | bytes 24580
  385.1 0.8 copy-start.1
  410.4 119.7 %copy-start.5 = (bf16[1,2048,768]{2,1,0:T(8,128)(2,1)S(1)}, bf16[1,2048,768]{2,1,0:T(8,128)(2,1)}, u32[]{:S(2)}) copy-start(bf16[1,2048,768]{2,1,0:T(8,128)(2,1)} %param.15) | copy-start | bytes 9437188
  530.2 4.3 copy-start.6
  545.4 5.4 copy-start.3
  545.4 120.4 %all-to-all-start.2 = ((bf16[16,80,2048]{2,1,0:T(8,128)(2,1)}), bf16[16,80,2048]{2,1,0:T(8,128)(2,1)}, u32[]{:S(2)}, u32[]{:S(2)}) async-start(bf16[16,80,2048]{2,1,0:T(8,128)(2,1)} %bitcast.44), calls=%async_computation.2 | async-start | bytes 10485760 | tf_op jit(solution)/shard_map/all_to_all | solution.py:46
